TPU v7x, 32 devices: a whole 2x2x4 slice. The times are simulated.
32 devices in a mesh: vocab: 16 (over z, y, core), tok: 2 (over x).
Axes of the slice: x: 2, y: 2, z: 4, core: 2. Of those that a mesh axis runs over, the one named last changes fastest.
Arguments:
- hidden: bfloat16 [2048, 4096], P('tok', 'vocab'), may hold values from -64 to 64
- weight: bfloat16 [4096, 16384], P(None, 'vocab'), may hold values from -1 to 1
- proj_in: bfloat16 [4096, 64], replicated, may hold values from -0.09375 to 0.09375
- proj_out: bfloat16 [16384, 64], P('vocab'), may hold values from -6 to 6
- targets: int32 [2048], P('tok'), may hold values from 0 to 16383
- segments: int32 [2, 1024], P('tok'), may hold values from 0 to 15, never falling along the last dimension, each value on 1 to 128 neighbouring positions
- queries: bfloat16 [2048, 4096], P(('vocab', 'tok')), may hold values from -0.059814453 to 0.059814453
Outputs:
- scores: float32 [32, 2048], P(None, ('vocab', 'tok'))
Inputs may be any that keep to these rules, and one draw needn't show every extreme that they name: `segments`: each group's row numbers its documents 0 to 15 in order, each with 1 to 128 tokens.
All inputs are finite; a program needn't handle non-finite values.
Results may differ from a plain program's by a relative error of at most 0.0095.
Values may be sent and summed in bfloat16 or wider, within the bound.
A program may use at most 64 MiB of HBM per device.

v0:
```python
import functools

import jax
import jax.numpy as jnp
from jax import lax
from jax.experimental import pallas as pl
from jax.experimental.pallas import tpu as pltpu
from jax.sharding import PartitionSpec as P

DOC_V = 1
MESH = pl.DeviceIdType.MESH
LANES = 128
ACROSS = (((1,), (1,)), ((), ()))


def chip_of(place, chips):
    back = place // (chips // 2)
    return (1 - back) * 2 * place + back * (2 * (chips - 1 - place) + 1)


def place_of(chip, chips):
    odd, half = chip % 2, chip // 2
    return odd * (chips - 1 - half) + (1 - odd) * half


def kernel(
    devices,
    groups,
    h_ref, w_hbm, pin_ref, po_ref, tgt_ref, seg_ref,
    out_ref,
    held, w_ref, logits, left, pa_ref, pb_ref, turned, spread, msg, stat, got_msg, got_stat,
    weights, right,
    w_sem, ring_send, ring_recv, mate_send, mate_recv, own_send, own_recv,
    msg_send, msg_recv, stat_send, stat_recv, right_send, right_recv,
    group_send, group_recv,
):
    chips, steps = devices // 2, devices // 4
    tokens, depth = h_ref.shape
    vocab = w_ref.shape[1]
    rank = pin_ref.shape[0]
    half_rows = tokens // 2
    block = half_rows // devices
    docs = out_ref.shape[0] // groups
    group = lax.axis_index("tok")
    me = lax.axis_index("vocab")
    core = me % 2
    place = place_of(me // 2, chips)
    mate = me + 1 - 2 * core
    nexts = [
        2 * chip_of((place + 1) % chips, chips) + core,
        2 * chip_of((place + chips - 1) % chips, chips) + core,
    ]

    barrier = pltpu.get_barrier_semaphore()
    for k in range(1, devices):
        pl.semaphore_signal(
            barrier, inc=1, device_id={"vocab": (me + k) % devices}, device_id_type=MESH
        )
    for k in range(1, groups):
        pl.semaphore_signal(
            barrier, inc=1, device_id={"tok": (group + k) % groups}, device_id_type=MESH
        )
    w_copy = pltpu.make_async_copy(w_hbm, w_ref, w_sem)
    w_copy.start()
    pl.semaphore_wait(barrier, devices + groups - 2)

    sent = []

    def remote(src, dst, send_sem, recv_sem, device, other=None):
        target = {"vocab": device} if other is None else {"tok": other}
        return pltpu.make_async_remote_copy(
            src_ref=src, dst_ref=dst, send_sem=send_sem, recv_sem=recv_sem,
            device_id=target, device_id_type=MESH,
        )

    def start(*args):
        copy = remote(*args)
        copy.start()
        sent.append(copy)

    def source_of(way, step):
        shift = (chips - step) if way == 0 else step
        return 2 * chip_of((place + shift) % chips, chips) + core

    def piece(slot, half):
        return held.at[slot, pl.ds(half * half_rows, half_rows), :]

    def own_piece(half):
        return h_ref.at[pl.ds(half * half_rows, half_rows), :]

    def travels(way, step, half):
        return step < steps - 1 or (step == steps - 1 and half == way)

    for half in range(2):
        for way in range(2):
            if travels(way, 0, half):
                start(
                    own_piece(half), piece(me, half),
                    ring_send.at[way, 0, half], ring_recv.at[way, 0, half], nexts[way],
                )
    for half in range(2):
        start(own_piece(half), piece(me, half), own_send.at[half], own_recv.at[half], mate)

    tile = 256 if tokens % 256 == 0 else tokens

    def consume(load, slot, first=False):
        deep = pl.ds(pl.multiple_of(slot * depth, depth), depth)

        def body(i, carry):
            rows = pl.ds(pl.multiple_of(i * tile, tile), tile)
            states = load(rows)
            value = jnp.dot(states, w_ref[deep, :], preferred_element_type=jnp.float32)
            side = lax.dot_general(
                states, pin_ref[:, deep], ACROSS, preferred_element_type=jnp.float32
            )
            if first:
                logits[rows, :] = value
                left[rows, 0:rank] = side
            else:
                logits[rows, :] += value
                left[rows, 0:rank] += side
            return carry

        lax.fori_loop(0, tokens // tile, body, 0)

    left[...] = jnp.zeros_like(left)
    pa_ref[...] = jnp.zeros_like(pa_ref)
    pb_ref[...] = jnp.zeros_like(pb_ref)
    pa_ref[0:rank, :] = po_ref[...]
    pb_ref[rank : 2 * rank, :] = po_ref[...]
    w_copy.wait()
    consume(lambda rows: h_ref[rows, :], me, first=True)
    for half in range(2):
        remote(
            own_piece(half), piece(mate, half), own_send.at[half], own_recv.at[half], mate
        ).wait_recv()
    consume(lambda rows: held[mate, rows, :], mate)

    flip = 1 - 2 * core

    def consume_mates(step):
        for half in range(2):
            for way in range(2):
                if travels(way, step, half):
                    there = piece(source_of(way, step + 1) + flip, half)
                    remote(
                        there, there, mate_send.at[way, step, half],
                        mate_recv.at[way, step, half], mate,
                    ).wait_recv()
        for slot in slots_of(step):
            consume(lambda rows, slot=slot: held[slot + flip, rows, :], slot + flip)

    def slots_of(step):
        return [source_of(way, step + 1) for way in range(2 if step < steps - 1 else 1)]

    for step in range(steps):
        for half in range(2):
            for way in range(2):
                if not travels(way, step, half):
                    continue
                slot = source_of(way, step + 1)
                here = piece(slot, half)
                remote(
                    here, here, ring_send.at[way, step, half],
                    ring_recv.at[way, step, half], nexts[way],
                ).wait_recv()
                if travels(way, step + 1, half):
                    start(
                        here, here, ring_send.at[way, step + 1, half],
                        ring_recv.at[way, step + 1, half], nexts[way],
                    )
                start(
                    here, here, mate_send.at[way, step, half],
                    mate_recv.at[way, step, half], mate,
                )
            if half == 0 and step > 0:
                consume_mates(step - 1)
        for slot in slots_of(step):
            consume(lambda rows, slot=slot: held[slot, rows, :], slot)
    consume_mates(steps - 1)

    lane = lax.broadcasted_iota(jnp.int32, (LANES, LANES), 1)
    column = lax.broadcasted_iota(jnp.int32, (LANES, vocab), 1)
    offset = me * vocab

    tiles = half_rows // LANES
    per_tile = LANES // block

    def soften(part, i):
        rows = pl.ds(pl.multiple_of(part * half_rows + i * LANES, LANES), LANES)
        value = logits[rows, :]
        top = jnp.max(value, axis=1, keepdims=True)
        expo = jnp.exp(value - top)
        wanted = jnp.broadcast_to(
            tgt_ref[:, rows].astype(jnp.float32), (LANES, LANES)
        )
        wanted = jnp.transpose(wanted)[:, 0:1].astype(jnp.int32)
        hit = column == wanted - offset
        rest = jnp.where(hit, 0.0, expo)
        total = jnp.sum(expo, axis=1, keepdims=True)
        others = jnp.sum(rest, axis=1, keepdims=True)
        onehot = jnp.where(hit, 1.0, 0.0).astype(jnp.bfloat16)
        both = lax.dot_general(
            rest.astype(jnp.bfloat16), pa_ref[...], ACROSS, preferred_element_type=jnp.float32
        )
        both += lax.dot_general(
            onehot, pb_ref[...], ACROSS, preferred_element_type=jnp.float32
        )
        spot = pl.ds(pl.multiple_of(i * LANES, LANES), LANES)
        msg[part, spot, :] = both.astype(jnp.bfloat16)
        return [top, total, others]

    def rows_of(device):
        return pl.ds(pl.multiple_of(device * block, block), block)

    def push(i):
        for d in range(per_tile):
            peer = i * per_tile + d
            away = (peer + devices - me) % devices

            @pl.when(peer != me)
            def _():
                remote(
                    stat.at[i], got_stat.at[me], stat_send.at[away], stat_recv.at[away], peer
                ).start()
                remote(
                    msg.at[:, rows_of(peer), :], got_msg.at[me],
                    msg_send.at[away], msg_recv.at[away], peer,
                ).start()

    first = me // per_tile + 1

    def stage(n, carry):
        i = (first + n) % tiles
        values = soften(0, i) + soften(1, i)
        packed = jnp.zeros((LANES, LANES), jnp.float32)
        for at, each in enumerate(values):
            packed = jnp.where(lane == at, each, packed)
        stat[i] = jnp.transpose(packed)[0:8, :]

        @pl.when(n > 0)
        def _():
            push((first + n + tiles - 1) % tiles)

        return carry

    lax.fori_loop(0, tiles, stage, 0)
    push((first + tiles - 1) % tiles)
    got_stat[me] = stat[me // per_tile]
    got_msg[me] = msg[:, rows_of(me), :]

    turned[...] = jnp.transpose(left[...])
    labels = seg_ref[...]
    member = labels == lax.broadcasted_iota(jnp.int32, (docs, tokens), 0)

    def mark(a, carry):
        rows = pl.ds(pl.multiple_of(a * docs, docs), docs)
        spread[rows, :] = jnp.where(member, turned[pl.ds(a, 1), :], 0.0).astype(jnp.bfloat16)
        return carry

    lax.fori_loop(0, rank, mark, 0)

    for k in range(1, devices):
        peer = (me + devices - k) % devices
        remote(
            got_stat.at[peer], got_stat.at[peer], stat_send.at[k], stat_recv.at[k], peer
        ).wait_recv()
    parts = []
    for p in range(2):
        tops = [got_stat[d, 3 * p : 3 * p + 1, :] for d in range(devices)]
        top = functools.reduce(jnp.maximum, tops)
        scale = [jnp.exp(each - top) for each in tops]
        total = sum(scale[d] * got_stat[d, 3 * p + 1 : 3 * p + 2, :] for d in range(devices))
        others = sum(scale[d] * got_stat[d, 3 * p + 2 : 3 * p + 3, :] for d in range(devices))
        weights[...] = jnp.zeros_like(weights)
        for d in range(devices):
            weights[d : d + 1, :] = scale[d] / total
        weights[devices : devices + 1, :] = others / total
        weights[...] = jnp.transpose(weights[...])
        parts.append(
            weights[pl.ds(pl.multiple_of((me % per_tile) * block, block), block), :]
        )

    for k in range(1, devices):
        peer = (me + devices - k) % devices
        remote(
            got_msg.at[peer], got_msg.at[peer], msg_send.at[k], msg_recv.at[k], peer
        ).wait_recv()
    results = []
    for p in range(2):
        summed = jnp.zeros((block, LANES), jnp.float32)
        plain = jnp.zeros((block, LANES), jnp.float32)
        for d in range(devices):
            value = got_msg[d, p].astype(jnp.float32)
            summed += value * parts[p][:, d : d + 1]
            plain += value
        results.append((summed, plain, parts[p][:, devices : devices + 1]))
    inside = lax.broadcasted_iota(jnp.int32, (block, LANES), 1) < rank
    (low, low_plain, low_share), (high, high_plain, high_share) = results
    low = low - low_share * pltpu.roll(low_plain, rank, 1)
    high = pltpu.roll(high, rank, 1) - high_share * high_plain
    right[rows_of(me), :] = jnp.where(inside, low, high).astype(jnp.bfloat16)
    for k in range(1, devices):
        start(
            right.at[rows_of(me), :], right.at[rows_of(me), :],
            right_send.at[k], right_recv.at[k], (me + k) % devices,
        )
    for k in range(1, devices):
        peer = (me + devices - k) % devices
        remote(
            right.at[rows_of(peer), :], right.at[rows_of(peer), :],
            right_send.at[k], right_recv.at[k], peer,
        ).wait_recv()

    mine = pl.ds(pl.multiple_of(group * docs, docs), docs)
    height = 8 * docs
    side = lax.broadcasted_iota(jnp.int32, (docs, LANES), 1) < rank
    for n in range(rank // 8):
        rows = pl.ds(n * height, height)
        early = jnp.dot(
            spread[rows, 0:half_rows], right[...], preferred_element_type=jnp.float32
        )
        late = jnp.dot(
            spread[rows, half_rows:tokens], right[...], preferred_element_type=jnp.float32
        )
        for a in range(0, 8, 2):
            even, odd = slice(a * docs, (a + 1) * docs), slice((a + 1) * docs, (a + 2) * docs)
            value = jnp.where(
                side,
                early[even] + pltpu.roll(late[even], rank, 1),
                pltpu.roll(early[odd], rank, 1) + late[odd],
            )
            at = (n * 8 + a) // 2 * LANES
            out_ref[mine, at : at + LANES] = value.astype(jnp.bfloat16)
    for k in range(1, groups):
        start(
            out_ref.at[mine, :], out_ref.at[mine, :],
            group_send.at[k], group_recv.at[k], None, (group + k) % groups,
        )
    for k in range(1, groups):
        other = (group + groups - k) % groups
        theirs = out_ref.at[pl.ds(pl.multiple_of(other * docs, docs), docs), :]
        remote(
            theirs, theirs, group_send.at[k], group_recv.at[k], None, other
        ).wait_recv()
    for k in range(1, devices):
        peer = (me + k) % devices
        remote(
            stat.at[peer // per_tile], got_stat.at[me], stat_send.at[k], stat_recv.at[k], peer
        ).wait_send()
        remote(
            msg.at[:, rows_of(peer), :], got_msg.at[me], msg_send.at[k], msg_recv.at[k], peer
        ).wait_send()
    for copy in sent:
        copy.wait_send()


def document_grads(devices, groups, hidden, weight, proj_in, proj_out, targets, segments):
    tokens, depth = hidden.shape
    width, vocab = weight.shape
    rank = proj_in.shape[1]
    docs = DOC_V * devices
    steps = devices // 4
    block = tokens // (2 * devices)
    vmem = pl.BlockSpec(memory_space=pltpu.VMEM)
    dma = pltpu.SemaphoreType.DMA
    ring = dma((2, steps, 2))
    peers = dma((devices,))
    return pl.pallas_call(
        functools.partial(kernel, devices, groups),
        out_shape=jax.ShapeDtypeStruct((groups * docs, rank * rank), jnp.bfloat16),
        in_specs=[vmem, pl.BlockSpec(memory_space=pl.ANY)] + [vmem] * 4,
        out_specs=vmem,
        scratch_shapes=[
            pltpu.VMEM((devices, tokens, depth), jnp.bfloat16),
            pltpu.VMEM((width, vocab), jnp.bfloat16),
            pltpu.VMEM((tokens, vocab), jnp.float32),
            pltpu.VMEM((tokens, LANES), jnp.float32),
            pltpu.VMEM((LANES, vocab), jnp.bfloat16),
            pltpu.VMEM((LANES, vocab), jnp.bfloat16),
            pltpu.VMEM((LANES, tokens), jnp.float32),
            pltpu.VMEM((docs * rank, tokens), jnp.bfloat16),
            pltpu.VMEM((2, tokens // 2, LANES), jnp.bfloat16),
            pltpu.VMEM((tokens // 2 // LANES, 8, LANES), jnp.float32),
            pltpu.VMEM((devices, 2, block, LANES), jnp.bfloat16),
            pltpu.VMEM((devices, 8, LANES), jnp.float32),
            pltpu.VMEM((LANES, LANES), jnp.float32),
            pltpu.VMEM((tokens // 2, LANES), jnp.bfloat16),
            dma(()), ring, ring, ring, ring, dma((2,)), dma((2,)),
            peers, peers, peers, peers, peers, peers, dma((groups,)), dma((groups,)),
        ],
        compiler_params=pltpu.CompilerParams(
            collective_id=0, has_side_effects=True, vmem_limit_bytes=60 * 1024 * 1024
        ),
    )(
        hidden, weight, proj_in.T, proj_out.T, targets[None, :], segments,
    )


def solution(mesh):
    devices, groups = mesh.shape["vocab"], mesh.shape["tok"]

    def per_device(hidden, weight, proj_in, proj_out, targets, segments, queries):
        grads = document_grads(
            devices, groups, hidden, weight, proj_in, proj_out, targets, segments
        )
        return lax.dot_general(
            grads,
            queries,
            (((1,), (1,)), ((), ())),
            preferred_element_type=jnp.float32,
        )

    return jax.shard_map(
        per_device,
        mesh=mesh,
        in_specs=(
            P("tok", "vocab"),
            P(None, "vocab"),
            P(),
            P("vocab", None),
            P("tok"),
            P("tok", None),
            P(("vocab", "tok"), None),
        ),
        out_specs=P(None, ("vocab", "tok")),
        check_vma=False,
    )
```

profile of v0, /device:TPU:0, one launch (start us, length us, event | category | flops | bytes accessed | tf_op | source)
XLA Modules:
  0.0 80.4 jit_solution(16827783383900479003)
XLA Ops:
  0.0 0.0 copy-start
  0.0 78.5 %shard_map.73 = bf16[32,4096]{1,0:T(8,128)(2,1)} custom-call(bf16[1024,256]{1,0:T(8,128)(2,1)} %h_ref.1, bf16[4096,1024]{1,0:T(8,128)(2,1)} %w_hbm.1, bf16[64,4096]{1,0:T(8,128)(2,1)} %bitcast.5, bf16[64,1024]{1,0:T(8,128)(2,1)} %bitcast.6, s32[1,1024]{1,0:T(1,128)} %bitcast.7, s32[1,1024]{1,0:T(1,128)} %seg_ref.1), custom_call_target="tpu_custom_call" | custom-call | tf_op jit(solution)/shard_map/pallas_call | solution.py:369
  78.6 0.0 copy-done
  78.6 1.8 %fusion = f32[32,64]{1,0:T(8,128)} fusion(bf16[32,4096]{1,0:T(8,128)(2,1)} %shard_map.73, bf16[64,4096]{1,0:T(8,128)(2,1)S(1)} %copy-done), kind=kOutput, calls=%fused_computation | convolution fusion | flops 16777216 | bytes 794624 | tf_op jit(solution)/shard_map/dot_general | solution.py:407
Async XLA Ops:
  0.0 78.6 %copy-start = (bf16[64,4096]{1,0:T(8,128)(2,1)S(1)}, bf16[64,4096]{1,0:T(8,128)(2,1)}, u32[]{:S(2)}) copy-start(bf16[64,4096]{1,0:T(8,128)(2,1)} %param.13) | copy-start | bytes 1572868
where the time goes:
time: 80.6 us; the launch traced here: 80.4 us
  Pallas kernels  78.5 us (97%)
  matrix products  1.83 us (2%)
    pallas_call x1, Pallas kernels, document_grads(): pl.pallas_call(functools.partial(kernel, devices, groups), out_shape=jax....  78.5 us
    dot_general x1, matrix products, per_device(): lax.dot_general(grads, queries, (((1,), (1,)), ((), ())), preferred_eleme...  1.83 us

commit v1 on v0

v1 whole, which is shorter than its diff:
```python
import functools

import jax
import jax.numpy as jnp
from jax import lax
from jax.experimental import pallas as pl
from jax.experimental.pallas import tpu as pltpu
from jax.sharding import PartitionSpec as P

DOC_V = 1
MESH = pl.DeviceIdType.MESH
LANES = 128
BLOCK = 16
AHEAD = 2
ACROSS = (((1,), (1,)), ((), ()))


def chip_of(place, chips):
    back = place // (chips // 2)
    return (1 - back) * 2 * place + back * (2 * (chips - 1 - place) + 1)


def place_of(chip, chips):
    odd, half = chip % 2, chip // 2
    return odd * (chips - 1 - half) + (1 - odd) * half


def wavefront(chunks, steps):
    order = [(c, 0) for c in range(min(AHEAD, chunks))]
    for k in range(chunks + steps):
        if AHEAD + k < chunks:
            order.append((AHEAD + k, 0))
        for s in range(1, steps):
            if 0 <= k + 1 - s < chunks:
                order.append((k + 1 - s, s))
    return order


def kernel(
    devices, groups, chunks,
    h_hbm, w_hbm, pin_hbm, po_hbm, tgt_hbm, seg_hbm, q_hbm,
    out_ref,
    h_ref, held, w_ref, pin_ref, po_ref, tgt_ref, seg_ref, qs, logits, left, shift, pb_ref, pa_ref,
    hot, turned, spread, msg, stat, got_mate, got_pack, comb, small, got_msg, got_stat,
    rights, grads, flat, scores,
    load_sem, ring_send, ring_recv, mate_send, mate_recv, own_send, own_recv,
    pair_send, pair_recv, msg_send, msg_recv, stat_send, stat_recv, right_send, right_recv,
    q_send, q_recv, group_send, group_recv,
):
    chips, steps = devices // 2, devices // 4
    tokens, depth = h_ref.shape
    vocab = w_ref.shape[1]
    rank = po_ref.shape[0]
    size = tokens // chunks
    half = size // 2
    block = half // chips
    docs = out_ref.shape[0] // groups
    number = out_ref.shape[1]
    group = lax.axis_index("tok")
    me = lax.axis_index("vocab")
    core = me % 2
    chip = me // 2
    place = place_of(chip, chips)
    mate = me + 1 - 2 * core
    nexts = [
        2 * chip_of((place + 1) % chips, chips) + core,
        2 * chip_of((place + chips - 1) % chips, chips) + core,
    ]

    loads = []
    for n, (src, dst) in enumerate([
        (h_hbm, h_ref), (tgt_hbm, tgt_ref), (po_hbm, po_ref), (w_hbm, w_ref), (pin_hbm, pin_ref),
        (seg_hbm, seg_ref), (q_hbm, qs.at[0]),
    ]):
        loads.append(pltpu.make_async_copy(src, dst, load_sem.at[n]))
    h_load, tgt_load, po_load, w_load, pin_load, seg_load, q_load = loads
    h_load.start()

    barrier = pltpu.get_barrier_semaphore()
    for device in nexts + [mate]:
        pl.semaphore_signal(
            barrier, inc=1, device_id={"vocab": device}, device_id_type=MESH
        )
    for k in range(1, groups):
        pl.semaphore_signal(
            barrier, inc=1, device_id={"tok": (group + k) % groups}, device_id_type=MESH
        )
    for each in loads[1:]:
        each.start()
    h_load.wait()
    pl.semaphore_wait(barrier, groups + 2)

    sent = []

    def remote(src, dst, send_sem, recv_sem, device, other=None):
        target = {"vocab": device} if other is None else {"tok": other}
        return pltpu.make_async_remote_copy(
            src_ref=src, dst_ref=dst, send_sem=send_sem, recv_sem=recv_sem,
            device_id=target, device_id_type=MESH,
        )

    def start(*args):
        copy = remote(*args)
        copy.start()
        sent.append(copy)

    def source_of(way, step):
        hops = (chips - step) if way == 0 else step
        return 2 * chip_of((place + hops) % chips, chips) + core

    def rows_of(c, s, way):
        if s == steps - 1:
            return pl.ds(c * size + way * half, half)
        return pl.ds(c * size, size)

    def piece(slot, c, s, way):
        return held.at[slot, rows_of(c, s, way), :]

    def begin(c):
        for way in range(2):
            start(
                h_ref.at[rows_of(c, 0, way), :], piece(me, c, 0, way),
                ring_send.at[way, 0, c], ring_recv.at[way, 0, c], nexts[way],
            )

    def arrive(c, s):
        for way in range(2):
            slot = source_of(way, s + 1)
            here = piece(slot, c, s, way)
            remote(
                here, here, ring_send.at[way, s, c], ring_recv.at[way, s, c], nexts[way]
            ).wait_recv()
            if s + 1 < steps:
                on = piece(slot, c, s + 1, way)
                start(
                    on, on, ring_send.at[way, s + 1, c], ring_recv.at[way, s + 1, c], nexts[way]
                )
            start(here, here, mate_send.at[way, s, c], mate_recv.at[way, s, c], mate)

    def own(c):
        rows = pl.ds(c * size, size)
        return h_ref.at[rows, :], held.at[me, rows, :], own_send.at[c], own_recv.at[c], mate

    wide = 512 if vocab % 512 == 0 else vocab

    def consume(c, loaders, first=False):
        rows = pl.ds(c * size, size)

        def body(n, carry):
            cols = pl.ds(pl.multiple_of(n * wide, wide), wide)
            value = 0.0 if first else logits[rows, cols]
            for load, slot in loaders:
                deep = pl.ds(pl.multiple_of(slot * depth, depth), depth)
                value += jnp.dot(load(rows), w_ref[deep, cols], preferred_element_type=jnp.float32)
            logits[rows, cols] = value
            return carry

        lax.fori_loop(0, vocab // wide, body, 0)
        side = 0.0 if first else left[rows, 0:rank]
        for load, slot in loaders:
            deep = pl.ds(pl.multiple_of(slot * depth, depth), depth)
            side += lax.dot_general(
                load(rows), pin_ref[:, deep], ACROSS, preferred_element_type=jnp.float32
            )
        left[rows, 0:rank] = side

    def consume_own(c):
        remote(*own(c)).wait_recv()
        consume(
            c,
            [(lambda rows: h_ref[rows, :], me), (lambda rows: held[mate, rows, :], mate)],
            first=True,
        )

    def consume_step(c, s):
        flip = 1 - 2 * core
        for way in range(2):
            there = piece(source_of(way, s + 1) + flip, c, s, way)
            remote(
                there, there, mate_send.at[way, s, c], mate_recv.at[way, s, c], mate
            ).wait_recv()
        loaders = []
        for way in range(2 if s < steps - 1 else 1):
            slot = source_of(way, s + 1)
            for each in (slot, slot + flip):
                loaders.append((lambda rows, each=each: held[each, rows, :], each))
        consume(c, loaders)

    lane = lax.broadcasted_iota(jnp.int32, (LANES, LANES), 1)
    inside = lane < rank
    base = lax.broadcasted_iota(jnp.int32, (LANES, vocab), 1) // LANES * LANES

    def spread_lanes(value):
        return jnp.concatenate([value] * (vocab // LANES), axis=1)

    def prepare():
        pa_ref[...] = jnp.zeros_like(pa_ref)
        pb_ref[...] = jnp.zeros_like(pb_ref)
        left[...] = jnp.zeros_like(left)
        grads[...] = jnp.zeros_like(grads)
        tgt_load.wait()
        po_load.wait()
        pa_ref[0:rank, :] = po_ref[...]
        pb_ref[rank : 2 * rank, :] = po_ref[...]

        def mark(i, carry):
            rows = pl.ds(pl.multiple_of(i * LANES, LANES), LANES)
            wanted = jnp.broadcast_to(tgt_ref[:, rows].astype(jnp.float32), (LANES, LANES))
            wanted = jnp.transpose(wanted).astype(jnp.int32) - me * vocab - lane
            shift[rows, :] = wanted
            onehot = jnp.where(spread_lanes(wanted) == base, 1.0, 0.0).astype(jnp.bfloat16)
            hot[rows, :] = lax.dot_general(
                onehot, pb_ref[...], ACROSS, preferred_element_type=jnp.float32
            )
            return carry

        lax.fori_loop(0, tokens // LANES, mark, 0)

    tiles = half // LANES

    def pair_copies(c, part):
        mine = pl.ds(pl.multiple_of(part * half, LANES), half)
        return [
            (msg.at[c, mine, :], got_mate.at[c], pair_send.at[0, c], pair_recv.at[0, c], mate),
            (stat.at[c, mine, :], got_pack.at[c], pair_send.at[1, c], pair_recv.at[1, c], mate),
        ]

    def pack(values):
        packed = jnp.zeros((LANES, LANES), jnp.float32)
        for at, each in enumerate(values):
            packed = jnp.where(lane == at, each, packed)
        return packed

    def soften(c, part):
        def tile(i, carry):
            spot = pl.ds(pl.multiple_of(part * half + i * LANES, LANES), LANES)
            rows = pl.ds(pl.multiple_of(c * size + part * half + i * LANES, LANES), LANES)
            value = logits[rows, :]
            top = jnp.max(value, axis=1, keepdims=True)
            expo = jnp.exp(value - top)
            rest = jnp.where(spread_lanes(shift[rows, :]) == base, 0.0, expo)
            total = jnp.sum(expo, axis=1, keepdims=True)
            others = jnp.sum(rest, axis=1, keepdims=True)
            both = hot[rows, :] + lax.dot_general(
                rest.astype(jnp.bfloat16), pa_ref[...], ACROSS,
                preferred_element_type=jnp.float32,
            )
            msg[c, spot, :] = both.astype(jnp.bfloat16)
            stat[c, spot, :] = pack([top, total, others])
            return carry

        lax.fori_loop(0, tiles, tile, 0)

    def soften_mate(c):
        soften(c, 1 - core)
        for copy in pair_copies(c, 1 - core):
            start(*copy)

    def soften_own(c):
        soften(c, core)

    def rs_copies(c, there):
        peer = 2 * there + core
        away = (there + chips - chip) % chips
        rows = pl.ds(pl.multiple_of(there * block, block), block)
        return [
            (comb.at[c, rows, :], got_msg.at[c, chip], msg_send.at[c, away], msg_recv.at[c, away],
             peer),
            (small.at[c, there], got_stat.at[c, chip], stat_send.at[c, away],
             stat_recv.at[c, away], peer),
        ]

    def join(c):
        for copy in pair_copies(c, core):
            remote(*copy).wait_recv()
        row = lax.broadcasted_iota(jnp.int32, (8, LANES), 0)
        spot = lax.broadcasted_iota(jnp.int32, (8, LANES), 1) // block
        keep = jnp.logical_and(row == spot, row < 3)
        per = LANES // block
        for i in range(tiles):
            at = pl.ds(i * LANES, LANES)
            rows = pl.ds(pl.multiple_of(core * half + i * LANES, LANES), LANES)
            a, b = stat[c, rows, :], got_pack[c, at, :]
            top = jnp.maximum(a[:, 0:1], b[:, 0:1])
            sa, sb = jnp.exp(a[:, 0:1] - top), jnp.exp(b[:, 0:1] - top)
            total = sa * a[:, 1:2] + sb * b[:, 1:2]
            others = sa * a[:, 2:3] + sb * b[:, 2:3]
            both = (
                jnp.where(inside, sa, 1.0) * msg[c, rows, :].astype(jnp.float32)
                + jnp.where(inside, sb, 1.0) * got_mate[c, at, :].astype(jnp.float32)
            )
            comb[c, at, :] = both.astype(jnp.bfloat16)
            line = jnp.transpose(pack([top, total, others]))[0:8, :]
            line = pltpu.roll(line, 0, 1, stride=block, stride_axis=0)
            for k in range(per):
                turn = pltpu.roll(line, (LANES - k * block) % LANES, 1)
                small[c, i * per + k] = jnp.sum(
                    jnp.where(keep, turn, 0.0), axis=0, keepdims=True
                )
        for k in range(1, chips):
            for copy in rs_copies(c, (chip + k) % chips):
                remote(*copy).start()
        got_msg[c, chip] = comb[c, pl.ds(pl.multiple_of(chip * block, block), block), :]
        got_stat[c, chip] = small[c, chip]

    place_in = core * chips + chip

    def gather_copy(c, k):
        peer = (me + k) % devices
        spot = rights.at[c, place_in]
        return spot, spot, right_send.at[c, k], right_recv.at[c, k], peer

    def reduce(c):
        for k in range(1, chips):
            there = (chip + chips - k) % chips
            for dst, send, recv in (
                (got_msg.at[c, there], msg_send.at[c, k], msg_recv.at[c, k]),
                (got_stat.at[c, there], stat_send.at[c, k], stat_recv.at[c, k]),
            ):
                remote(dst, dst, send, recv, 2 * there + core).wait_recv()
        lines = jnp.concatenate([got_stat[c, d] for d in range(chips)], axis=0)
        top = jnp.max(lines, axis=0, keepdims=True)
        scale = jnp.exp(lines - top)
        total = jnp.sum(scale * pltpu.roll(lines, LANES - block, 1), axis=0, keepdims=True)
        others = jnp.sum(scale * pltpu.roll(lines, LANES - 2 * block, 1), axis=0, keepdims=True)
        table = jnp.concatenate(
            [
                scale / total,
                jnp.broadcast_to(others / total, (8, LANES)),
                jnp.zeros((LANES - chips - 8, LANES), jnp.float32),
            ],
            axis=0,
        )
        table = jnp.transpose(table)[0:block, :]
        summed = jnp.zeros((block, LANES), jnp.float32)
        plain = jnp.zeros((block, LANES), jnp.float32)
        for d in range(chips):
            value = got_msg[c, d].astype(jnp.float32)
            summed += value * table[:, d : d + 1]
            plain += value
        right = summed - table[:, chips : chips + 1] * pltpu.roll(plain, rank, 1)
        low, high = right[0 : block // 2, :], right[block // 2 : block, :]
        packed = jnp.where(inside[0 : block // 2, :], low, pltpu.roll(high, rank, 1))
        rights[c, place_in] = packed.astype(jnp.bfloat16)
        for k in range(1, devices):
            start(*gather_copy(c, k))

    def mark_docs(c):
        cols = pl.ds(c * size, size)
        turned[...] = jnp.transpose(left[cols, :])
        member = seg_ref[:, cols] == lax.broadcasted_iota(jnp.int32, (docs, size), 0)

        def body(p, carry):
            rows = pl.ds(pl.multiple_of(p * docs, docs), docs)
            for side in range(2):
                line = turned[pl.ds(2 * p + side, 1), :]
                spread[c, rows, side * size : (side + 1) * size] = jnp.where(
                    member, line, 0.0
                ).astype(jnp.bfloat16)
            return carry

        lax.fori_loop(0, rank // 2, body, 0)

    def add_docs(c):
        for k in range(1, devices):
            peer = (me + devices - k) % devices
            spot = rights.at[c, peer % 2 * chips + peer // 2]
            remote(spot, spot, right_send.at[c, k], right_recv.at[c, k], peer).wait_recv()
        part = block // 2
        packed = rights[c].astype(jnp.float32).reshape(devices * part, LANES)
        moved = pltpu.roll(packed, rank, 1)
        both = jnp.concatenate(
            [packed.reshape(devices, 1, part, LANES), moved.reshape(devices, 1, part, LANES)],
            axis=1,
        ).reshape(size, LANES)
        within = lax.broadcasted_iota(jnp.int32, (size, LANES), 1) < rank
        sides = jnp.concatenate(
            [jnp.where(within, both, 0.0), jnp.where(within, 0.0, pltpu.roll(both, rank, 1))],
            axis=0,
        ).astype(jnp.bfloat16)
        grads[...] += jnp.dot(spread[c], sides, preferred_element_type=jnp.float32)

    order = wavefront(chunks, steps)
    ahead = min(AHEAD, chunks)
    for c in range(ahead):
        begin(c)
    for c in range(chunks):
        start(*own(c))
    for k in range(1, groups):
        start(
            q_hbm, qs.at[groups - k], q_send.at[k], q_recv.at[k], None, (group + k) % groups
        )
    prepare()
    w_load.wait()
    pin_load.wait()
    seg_load.wait()
    for c in range(ahead):
        consume_own(c)

    extra = [functools.partial(consume_own, c) for c in range(ahead, chunks)]
    waiting, ends = [], []

    def finish(c):
        arrive(c, steps - 1)
        waiting.append((c, steps - 1))

    def work():
        while waiting:
            c, s = waiting.pop(0)
            consume_step(c, s)
            if s == steps - 1 and c < chunks - 1:
                extra.extend([
                    functools.partial(soften_mate, c), functools.partial(soften_own, c),
                    functools.partial(join, c), functools.partial(mark_docs, c),
                ])
        for _ in range(2):
            if extra:
                extra.pop(0)()

    for n, (c, s) in enumerate(order[ahead:]):
        if s == 0:
            begin(c)
            continue
        now = list(waiting)
        arrive(c, s - 1)
        work()
        waiting.append((c, s - 1))
        if s == steps - 1:
            ends.append((n + 2, c))
        while ends and ends[0][0] <= n and len(ends) > 1:
            finish(ends.pop(0)[1])
    last = chunks - 1
    while ends:
        finish(ends.pop(0)[1])
        if ends:
            work()
    while extra:
        extra.pop(0)()
    for c in range(max(last - 1, 0)):
        reduce(c)
    work()
    while extra:
        extra.pop(0)()
    soften_mate(last)
    soften_own(last)
    join(last)
    if last > 0:
        reduce(last - 1)
    mark_docs(last)
    for c in range(last):
        add_docs(c)
    reduce(last)
    q_load.wait()
    for k in range(1, groups):
        remote(
            qs.at[k], qs.at[k], q_send.at[groups - k], q_recv.at[groups - k], None,
            (group + k) % groups,
        ).wait_recv()
    add_docs(last)

    for p in range(rank // 2):
        flat[:, p * LANES : (p + 1) * LANES] = grads[p * docs : (p + 1) * docs, :].astype(
            jnp.bfloat16
        )
    mine = pl.ds(pl.multiple_of(group * docs, docs), docs)
    for k in [*range(1, groups), 0]:
        value = lax.dot_general(flat[...], qs[k], ACROSS, preferred_element_type=jnp.float32)
        if k == 0:
            out_ref[mine, :] = value
        else:
            scores[k] = value
            start(
                scores.at[k], out_ref.at[mine, :], group_send.at[k], group_recv.at[k], None,
                (group + k) % groups,
            )
    for k in range(1, groups):
        other = (group + groups - k) % groups
        theirs = out_ref.at[pl.ds(pl.multiple_of(other * docs, docs), docs), :]
        remote(
            theirs, theirs, group_send.at[k], group_recv.at[k], None, other
        ).wait_recv()
    for c in range(chunks):
        for k in range(1, chips):
            for copy in rs_copies(c, (chip + k) % chips):
                remote(*copy).wait_send()
    for copy in sent:
        copy.wait_send()


def attribution(devices, groups, hidden, weight, proj_in, proj_out, targets, segments, queries):
    tokens, depth = hidden.shape
    width, vocab = weight.shape
    rank = proj_in.shape[1]
    number = queries.shape[0]
    docs = DOC_V * devices
    chips, steps = devices // 2, devices // 4
    chunks = max(1, min(4, tokens // (2 * chips * BLOCK)))
    size = tokens // chunks
    half = size // 2
    block = half // chips
    hbm = pl.BlockSpec(memory_space=pl.ANY)
    dma = pltpu.SemaphoreType.DMA
    ring = dma((2, steps, chunks))
    once = dma((chunks,))
    pair = dma((2, chunks))
    peers = dma((chunks, chips))
    everyone = dma((chunks, devices))
    across = dma((groups,))
    f32, bf16 = jnp.float32, jnp.bfloat16
    return pl.pallas_call(
        functools.partial(kernel, devices, groups, chunks),
        out_shape=jax.ShapeDtypeStruct((groups * docs, number), f32),
        in_specs=[hbm] * 7,
        out_specs=pl.BlockSpec(memory_space=pltpu.VMEM),
        scratch_shapes=[
            pltpu.VMEM((tokens, depth), bf16),
            pltpu.VMEM((devices, tokens, depth), bf16),
            pltpu.VMEM((width, vocab), bf16),
            pltpu.VMEM((rank, width), bf16),
            pltpu.VMEM((rank, vocab), bf16),
            pltpu.VMEM((1, tokens), jnp.int32),
            pltpu.VMEM((1, tokens), jnp.int32),
            pltpu.VMEM((groups, number, rank * rank), bf16),
            pltpu.VMEM((tokens, vocab), f32),
            pltpu.VMEM((tokens, LANES), f32),
            pltpu.VMEM((tokens, LANES), jnp.int32),
            pltpu.VMEM((LANES, vocab), bf16),
            pltpu.VMEM((LANES, vocab), bf16),
            pltpu.VMEM((tokens, LANES), f32),
            pltpu.VMEM((LANES, size), f32),
            pltpu.VMEM((chunks, docs * rank // 2, 2 * size), bf16),
            pltpu.VMEM((chunks, size, LANES), bf16),
            pltpu.VMEM((chunks, size, LANES), f32),
            pltpu.VMEM((chunks, half, LANES), bf16),
            pltpu.VMEM((chunks, half, LANES), f32),
            pltpu.VMEM((chunks, half, LANES), bf16),
            pltpu.VMEM((chunks, chips, 1, LANES), f32),
            pltpu.VMEM((chunks, chips, block, LANES), bf16),
            pltpu.VMEM((chunks, chips, 1, LANES), f32),
            pltpu.VMEM((chunks, devices, block // 2, LANES), bf16),
            pltpu.VMEM((docs * rank // 2, LANES), f32),
            pltpu.VMEM((docs, rank * rank), bf16),
            pltpu.VMEM((groups, docs, number), f32),
            dma((7,)), ring, ring, ring, ring, once, once, pair, pair,
            peers, peers, peers, peers, everyone, everyone, across, across, across, across,
        ],
        compiler_params=pltpu.CompilerParams(
            collective_id=0, has_side_effects=True, vmem_limit_bytes=60 * 1024 * 1024
        ),
    )(
        hidden, weight, proj_in.T, proj_out.T, targets[None, :], segments, queries,
    )


def solution(mesh):
    devices, groups = mesh.shape["vocab"], mesh.shape["tok"]
    return jax.shard_map(
        functools.partial(attribution, devices, groups),
        mesh=mesh,
        in_specs=(
            P("tok", "vocab"),
            P(None, "vocab"),
            P(),
            P("vocab", None),
            P("tok"),
            P("tok", None),
            P(("vocab", "tok"), None),
        ),
        out_specs=P(None, ("vocab", "tok")),
        check_vma=False,
    )
```

time: 80.6 us -> 75 us (0.931)
  Pallas kernels: 78.5 us -> 73.4 us
  matrix products: 1.83 us -> 0 us
  local copies, waits for them, and re-layouts: 0.01 us -> 1.32 us
    pallas_call x1, Pallas kernels: 78.5 us -> 73.4 us  [attribution(): pl.pallas_call(functools.partial(kernel, devices, groups, chunks), out_sh...]
    dot_general x1 -> x0, matrix products: 1.83 us -> none  [per_device(): lax.dot_general(grads, queries, (((1,), (1,)), ((), ())), preferred_eleme...]
    unnamed x2 -> x1, local copies, waits for them, and re-layouts: 0.01 us -> 1.32 us
where the time goes in v1:
time: 75 us; the launch traced here: 74.8 us
  Pallas kernels  73.4 us (98%)
  local copies, waits for them, and re-layouts  1.32 us (2%)
    pallas_call x1, Pallas kernels, attribution(): pl.pallas_call(functools.partial(kernel, devices, groups, chunks), out_sh...  73.4 us

profile of v1, /device:TPU:0, one launch (start us, length us, event | category | flops | bytes accessed | tf_op | source)
XLA Modules:
  0.0 74.8 jit_solution(15520293224210699761)
XLA Ops:
  0.0 73.4 %shard_map.73 = f32[32,64]{1,0:T(8,128)} custom-call(bf16[1024,256]{1,0:T(8,128)(2,1)} %h_hbm.1, bf16[4096,1024]{1,0:T(8,128)(2,1)} %w_hbm.1, bf16[64,4096]{1,0:T(8,128)(2,1)} %bitcast.3, bf16[64,1024]{1,0:T(8,128)(2,1)} %bitcast.4, s32[1,1024]{1,0:T(1,128)} %bitcast.5, s32[1,1024]{1,0:T(1,128)} %seg_hbm.1, bf16[64,4096]{1,0:T(8,128)(2,1)} %q_hbm.1), custom_call_target="tpu_custom_call" | custom-call | tf_op jit(solution)/shard_map/pallas_call | solution.py:510
  73.4 1.3 %copy.9 = f32[32,64]{1,0:T(8,128)} copy(f32[32,64]{1,0:T(8,128)} %shard_map.73) | data formatting | bytes 16384

commit v2 on v1

v2 whole, which is shorter than its diff:
```python
import functools

import jax
import jax.numpy as jnp
from jax import lax
from jax.experimental import pallas as pl
from jax.experimental.pallas import tpu as pltpu
from jax.sharding import PartitionSpec as P

DOC_V = 1
MESH = pl.DeviceIdType.MESH
LANES = 128
BLOCK = 16
AHEAD = 2
HOLD = 5
ACROSS = (((1,), (1,)), ((), ()))


def chip_of(place, chips):
    back = place // (chips // 2)
    return (1 - back) * 2 * place + back * (2 * (chips - 1 - place) + 1)


def place_of(chip, chips):
    odd, half = chip % 2, chip // 2
    return odd * (chips - 1 - half) + (1 - odd) * half


def wavefront(chunks, steps):
    order = [(c, 0) for c in range(min(AHEAD, chunks))]
    for k in range(chunks + steps):
        if AHEAD + k < chunks:
            order.append((AHEAD + k, 0))
        for s in range(1, steps):
            if 0 <= k + 1 - s < chunks:
                order.append((k + 1 - s, s))
    return order


def kernel(
    devices, groups, chunks,
    h_hbm, w_hbm, pin_hbm, po_hbm, tgt_hbm, seg_hbm, q_hbm,
    out_ref,
    h_ref, held, w_ref, pin_ref, tgt_ref, seg_ref, qs, logits, left, shift, pb_ref, pa_ref,
    hot, turned, spread, msg, small, got_msg, got_stat, rights,
    hot_late, got_hot, hot_sum, msg_late, got_late, line_late, got_line, rights_late,
    grads, flat, scores,
    load_sem, ring_send, ring_recv, side_send, side_recv, own_send, own_recv,
    mate_send, mate_recv, left_send, left_recv,
    msg_send, msg_recv, stat_send, stat_recv, right_send, right_recv,
    late_send, late_recv, swap_send, swap_recv, q_send, q_recv, group_send, group_recv,
):
    chips, steps = devices // 2, devices // 4
    tokens, depth = h_ref.shape
    vocab = w_ref.shape[2]
    rank = po_hbm.shape[0]
    size = tokens // chunks
    half = size // 2
    block = half // chips
    docs = out_ref.shape[0] // groups
    number = out_ref.shape[1]
    last = chunks - 1
    group = lax.axis_index("tok")
    me = lax.axis_index("vocab")
    core = me % 2
    chip = me // 2
    place = place_of(chip, chips)
    mate = me + 1 - 2 * core
    nexts = [
        2 * chip_of((place + 1) % chips, chips) + core,
        2 * chip_of((place + chips - 1) % chips, chips) + core,
    ]

    my_cols = pl.ds(pl.multiple_of(core * vocab, vocab), vocab)
    pa_mine, pb_mine = pa_ref.at[0:rank, my_cols], pb_ref.at[rank : 2 * rank, my_cols]
    loads = []
    for n, (src, dst) in enumerate([
        (h_hbm, h_ref), (tgt_hbm, tgt_ref), (po_hbm, pa_mine), (po_hbm, pb_mine),
        (w_hbm, w_ref.at[core]), (pin_hbm, pin_ref), (seg_hbm, seg_ref), (q_hbm, qs.at[pl.ds(0, number), :]),
    ]):
        loads.append(pltpu.make_async_copy(src, dst, load_sem.at[n]))
    h_load, tgt_load, pa_load, pb_load, w_load, pin_load, seg_load, q_load = loads
    h_load.start()

    barrier = pltpu.get_barrier_semaphore()
    for device in nexts + [mate]:
        pl.semaphore_signal(
            barrier, inc=1, device_id={"vocab": device}, device_id_type=MESH
        )
    for k in range(1, groups):
        pl.semaphore_signal(
            barrier, inc=1, device_id={"tok": (group + k) % groups}, device_id_type=MESH
        )
    for each in loads[1:]:
        each.start()
    h_load.wait()
    pl.semaphore_wait(barrier, groups + 2)

    sent = []

    def remote(src, dst, send_sem, recv_sem, device, other=None):
        target = {"vocab": device} if other is None else {"tok": other}
        return pltpu.make_async_remote_copy(
            src_ref=src, dst_ref=dst, send_sem=send_sem, recv_sem=recv_sem,
            device_id=target, device_id_type=MESH,
        )

    def start(*args):
        copy = remote(*args)
        copy.start()
        sent.append(copy)

    def source_of(way, step):
        hops = (chips - step) if way == 0 else step
        return chip_of((place + hops) % chips, chips)

    def tokens_of(c, who):
        return pl.ds(pl.multiple_of(c * size + who * half, LANES), half)

    def piece(slot, c, s, way):
        if s == steps - 1:
            return held.at[slot, pl.ds(c * half + way * (half // 2), half // 2), :]
        return held.at[slot, pl.ds(c * half, half), :]

    def cols_of(who):
        return pl.ds(pl.multiple_of(who * depth, depth), depth)

    def own_part(c, way):
        return (
            h_ref.at[tokens_of(c, core), :],
            held.at[chip, pl.ds(c * half, half), cols_of(core)],
            side_send.at[way, c], side_recv.at[way, c], nexts[way],
        )

    def mate_part(c, way):
        part = held.at[chip, pl.ds(c * half, half), cols_of(1 - core)]
        return part, part, ring_send.at[way, 0, c], ring_recv.at[way, 0, c], nexts[way]

    def swap(c, who):
        return (
            h_ref.at[tokens_of(c, 1 - who), :],
            held.at[chip, pl.ds(c * half, half), cols_of(who)],
            own_send.at[c], own_recv.at[c], mate,
        )

    def begin(c):
        for way in range(2):
            start(*own_part(c, way))

    def begin_mate(c):
        remote(*swap(c, 1 - core)).wait_recv()
        for way in range(2):
            start(*mate_part(c, way))

    def arrive(c, s):
        for way in range(2):
            slot = source_of(way, s + 1)
            if s == 0:
                for who, send, recv in (
                    (core, side_send, side_recv.at[way, c]),
                    (1 - core, side_send, ring_recv.at[way, 0, c]),
                ):
                    here = held.at[slot, pl.ds(c * half, half), cols_of(who)]
                    remote(here, here, send.at[way, c], recv, nexts[way]).wait_recv()
            else:
                here = piece(slot, c, s, way)
                remote(
                    here, here, ring_send.at[way, s, c], ring_recv.at[way, s, c], nexts[way]
                ).wait_recv()
            if s + 1 < steps:
                on = piece(slot, c, s + 1, way)
                start(
                    on, on, ring_send.at[way, s + 1, c], ring_recv.at[way, s + 1, c], nexts[way]
                )

    wide = vocab
    per_core = vocab // wide

    def consume(c, loaders, first=False):
        rows = pl.ds(c * half, half)

        def body(n, carry):
            who = n // per_core
            cols = pl.ds(pl.multiple_of(n % per_core * wide, wide), wide)
            outs = pl.ds(pl.multiple_of(n * wide, wide), wide)
            value = 0.0 if first else logits[rows, outs]
            for load, deep in loaders:
                value += jnp.dot(
                    load(), w_ref[who, deep, cols], preferred_element_type=jnp.float32
                )
            logits[rows, outs] = value
            return carry

        lax.fori_loop(0, 2 * per_core, body, 0)
        side = 0.0 if first else left[c, core, :, 0:rank]
        for load, deep in loaders:
            side += lax.dot_general(
                load(), pin_ref[:, deep], ACROSS, preferred_element_type=jnp.float32
            )
        left[c, core, :, 0:rank] = side

    def deep_of(device):
        return pl.ds(pl.multiple_of(device * depth, depth), depth)

    def own_loaders(c):
        rows = pl.ds(c * half, half)
        return [
            (lambda: h_ref[tokens_of(c, core), :], deep_of(me)),
            (lambda: held[chip, rows, cols_of(1 - core)], deep_of(mate)),
        ]

    def step_loaders(c, s):
        rows = pl.ds(c * half, half)
        loaders = []
        for way in range(2 if s < steps - 1 else 1):
            slot = source_of(way, s + 1)
            deep = pl.ds(pl.multiple_of(slot * 2 * depth, 2 * depth), 2 * depth)
            loaders.append((lambda slot=slot: held[slot, rows, :], deep))
        return loaders

    lane = lax.broadcasted_iota(jnp.int32, (LANES, LANES), 1)
    inside = lane < rank
    base = lax.broadcasted_iota(jnp.int32, (LANES, 2 * vocab), 1) // LANES * LANES

    def spread_lanes(value):
        return jnp.concatenate([value] * (2 * vocab // LANES), axis=1)

    mates = [
        (pa_mine, pa_mine, mate_send.at[0], mate_recv.at[0], mate),
        (pb_mine, pb_mine, mate_send.at[1], mate_recv.at[1], mate),
        (w_hbm, w_ref.at[core], mate_send.at[2], mate_recv.at[2], mate),
    ]
    other_cols = pl.ds(pl.multiple_of((1 - core) * vocab, vocab), vocab)
    theirs = [
        pa_ref.at[0:rank, other_cols], pb_ref.at[rank : 2 * rank, other_cols],
        w_ref.at[1 - core],
    ]

    def from_mate(n):
        remote(theirs[n], theirs[n], mate_send.at[n], mate_recv.at[n], mate).wait_recv()

    def clear():
        pa_ref[rank : 2 * rank, :] = jnp.zeros((rank, 2 * vocab), jnp.bfloat16)
        pb_ref[0:rank, :] = jnp.zeros((rank, 2 * vocab), jnp.bfloat16)
        for c in range(chunks):
            left[c, core] = jnp.zeros((half, LANES), jnp.float32)
        grads[...] = jnp.zeros_like(grads)

    def prepare(c):
        for i in range(tiles):
            rows = pl.ds(c * half + i * LANES, LANES)
            spot = pl.ds(pl.multiple_of(c * size + core * half + i * LANES, LANES), LANES)
            wanted = jnp.broadcast_to(tgt_ref[:, spot].astype(jnp.float32), (LANES, LANES))
            wanted = jnp.transpose(wanted).astype(jnp.int32) - 2 * chip * vocab - lane
            shift[rows, :] = wanted
            onehot = jnp.where(spread_lanes(wanted) == base, 1.0, 0.0).astype(jnp.bfloat16)
            hot[rows, :] = lax.dot_general(
                onehot, pb_ref[...], ACROSS, preferred_element_type=jnp.float32
            )

    tiles = half // LANES

    def pack(values):
        packed = jnp.zeros((LANES, LANES), jnp.float32)
        for at, each in enumerate(values):
            packed = jnp.where(lane == at, each, packed)
        return packed

    def left_copy(c, who):
        return left.at[c, who], left.at[c, who], left_send.at[c], left_recv.at[c], mate

    def rs_copies(c, there):
        peer = 2 * there + core
        away = (there + chips - chip) % chips
        rows = pl.ds(pl.multiple_of(there * block, block), block)
        return [
            (msg.at[c, rows, :], got_msg.at[c, chip], msg_send.at[c, away], msg_recv.at[c, away],
             peer),
            (small.at[c, there], got_stat.at[c, chip], stat_send.at[c, away],
             stat_recv.at[c, away], peer),
        ]

    def soften(c):
        start(*left_copy(c, core))
        row = lax.broadcasted_iota(jnp.int32, (8, LANES), 0)
        spot = lax.broadcasted_iota(jnp.int32, (8, LANES), 1) // block
        keep = jnp.logical_and(row == spot, row < 3)
        per = LANES // block
        for i in range(tiles):
            rows = pl.ds(c * half + i * LANES, LANES)
            value = logits[rows, :]
            top = jnp.max(value, axis=1, keepdims=True)
            expo = jnp.exp(value - top)
            rest = jnp.where(spread_lanes(shift[rows, :]) == base, 0.0, expo)
            total = jnp.sum(expo, axis=1, keepdims=True)
            others = jnp.sum(rest, axis=1, keepdims=True)
            both = hot[rows, :] + lax.dot_general(
                rest.astype(jnp.bfloat16), pa_ref[...], ACROSS,
                preferred_element_type=jnp.float32,
            )
            msg[c, i * LANES : (i + 1) * LANES, :] = both.astype(jnp.bfloat16)
            line = jnp.transpose(pack([top, total, others]))[0:8, :]
            line = pltpu.roll(line, 0, 1, stride=block, stride_axis=0)
            for k in range(per):
                turn = pltpu.roll(line, (LANES - k * block) % LANES, 1)
                small[c, i * per + k] = jnp.sum(
                    jnp.where(keep, turn, 0.0), axis=0, keepdims=True
                )
        for k in range(1, chips):
            for copy in rs_copies(c, (chip + k) % chips):
                remote(*copy).start()
        got_msg[c, chip] = msg[c, pl.ds(pl.multiple_of(chip * block, block), block), :]
        got_stat[c, chip] = small[c, chip]

    fold = half // 2
    beside = lax.broadcasted_iota(jnp.int32, (fold, LANES), 1) < rank
    late = [(hot_late, got_hot), (msg_late, got_late), (line_late, got_line)]

    def late_copy(n, k):
        src, dst = late[n]
        there = (chip + k) % chips
        return src, dst.at[chip], late_send.at[n, k], late_recv.at[n, k], 2 * there + core

    def late_wait(n):
        for k in range(1, chips):
            there = (chip + chips - k) % chips
            spot = late[n][1].at[there]
            remote(
                spot, spot, late_send.at[n, k], late_recv.at[n, k], 2 * there + core
            ).wait_recv()

    def late_push(n):
        for k in range(1, chips):
            start(*late_copy(n, k))
        late[n][1][chip] = late[n][0][...]

    def push_hot():
        upper = hot[last * half : last * half + fold, :]
        lower = hot[last * half + fold : (last + 1) * half, :]
        hot_late[...] = jnp.where(beside, pltpu.roll(upper, rank, 1), lower).astype(jnp.bfloat16)
        late_push(0)

    def sum_hot():
        late_wait(0)
        value = jnp.zeros((fold, LANES), jnp.float32)
        for d in range(chips):
            value += got_hot[d].astype(jnp.float32)
        hot_sum[...] = value

    def soften_late():
        start(*left_copy(last, core))
        sums = []
        for i in range(tiles):
            rows = pl.ds(last * half + i * LANES, LANES)
            value = logits[rows, :]
            top = jnp.max(value, axis=1, keepdims=True)
            expo = jnp.exp(value - top)
            rest = jnp.where(spread_lanes(shift[rows, :]) == base, 0.0, expo)
            total = jnp.sum(expo, axis=1, keepdims=True)
            others = jnp.sum(rest, axis=1, keepdims=True)
            sums.append(lax.dot_general(
                rest.astype(jnp.bfloat16), pa_ref[...], ACROSS,
                preferred_element_type=jnp.float32,
            ))
            line_late[i] = jnp.transpose(pack([top, total, others]))[0:8, :]
        late_push(2)
        value = jnp.concatenate(sums, axis=0)
        msg_late[...] = jnp.where(
            beside, value[0:fold, :], pltpu.roll(value[fold:half, :], rank, 1)
        ).astype(jnp.bfloat16)
        late_push(1)

    def late_swap(who):
        return rights_late.at[who], rights_late.at[who], swap_send, swap_recv, mate

    def settle_late():
        late_wait(2)
        tables = []
        for i in range(tiles):
            lines = [got_line[d, i] for d in range(chips)]
            top = functools.reduce(jnp.maximum, [each[0:1, :] for each in lines])
            scale = [jnp.exp(each[0:1, :] - top) for each in lines]
            total = sum(scale[d] * lines[d][1:2, :] for d in range(chips))
            others = sum(scale[d] * lines[d][2:3, :] for d in range(chips))
            table = jnp.concatenate(
                [each / total for each in scale]
                + [
                    jnp.broadcast_to(others / total, (8, LANES)),
                    jnp.zeros((LANES - chips - 8, LANES), jnp.float32),
                ],
                axis=0,
            )
            tables.append(jnp.transpose(table))
        table = jnp.concatenate(tables, axis=0)

        def column(d):
            return jnp.where(beside, table[0:fold, d : d + 1], table[fold:half, d : d + 1])

        right = -column(chips) * hot_sum[...]
        factors = [column(d) for d in range(chips)]
        late_wait(1)
        for d in range(chips):
            right += factors[d] * got_late[d].astype(jnp.float32)
        rights_late[core] = right.astype(jnp.bfloat16)
        start(*late_swap(core))

    place_in = core * chips + chip

    def gather_copy(c, k):
        peer = (me + k) % devices
        spot = rights.at[c, place_in]
        return spot, spot, right_send.at[c, k], right_recv.at[c, k], peer

    def reduce(c):
        for k in range(1, chips):
            there = (chip + chips - k) % chips
            for dst, send, recv in (
                (got_msg.at[c, there], msg_send.at[c, k], msg_recv.at[c, k]),
                (got_stat.at[c, there], stat_send.at[c, k], stat_recv.at[c, k]),
            ):
                remote(dst, dst, send, recv, 2 * there + core).wait_recv()
        lines = jnp.concatenate([got_stat[c, d] for d in range(chips)], axis=0)
        top = jnp.max(lines, axis=0, keepdims=True)
        scale = jnp.exp(lines - top)
        total = jnp.sum(scale * pltpu.roll(lines, LANES - block, 1), axis=0, keepdims=True)
        others = jnp.sum(scale * pltpu.roll(lines, LANES - 2 * block, 1), axis=0, keepdims=True)
        table = jnp.concatenate(
            [
                scale / total,
                jnp.broadcast_to(others / total, (8, LANES)),
                jnp.zeros((LANES - chips - 8, LANES), jnp.float32),
            ],
            axis=0,
        )
        table = jnp.transpose(table)[0:block, :]
        summed = jnp.zeros((block, LANES), jnp.float32)
        plain = jnp.zeros((block, LANES), jnp.float32)
        for d in range(chips):
            value = got_msg[c, d].astype(jnp.float32)
            summed += value * table[:, d : d + 1]
            plain += value
        right = summed - table[:, chips : chips + 1] * pltpu.roll(plain, rank, 1)
        low, high = right[0 : block // 2, :], right[block // 2 : block, :]
        packed = jnp.where(inside[0 : block // 2, :], low, pltpu.roll(high, rank, 1))
        rights[c, place_in] = packed.astype(jnp.bfloat16)
        for k in range(1, devices):
            start(*gather_copy(c, k))

    def mark_docs(c):
        cols = pl.ds(c * size, size)
        remote(*left_copy(c, 1 - core)).wait_recv()
        turned[...] = jnp.transpose(left[c].reshape(size, LANES))
        member = seg_ref[:, cols] == lax.broadcasted_iota(jnp.int32, (docs, size), 0)

        def body(p, carry):
            rows = pl.ds(pl.multiple_of(p * docs, docs), docs)
            for side in range(2):
                line = turned[pl.ds(2 * p + side, 1), :]
                spread[c, rows, side * size : (side + 1) * size] = jnp.where(
                    member, line, 0.0
                ).astype(jnp.bfloat16)
            return carry

        lax.fori_loop(0, rank // 2, body, 0)

    def add_docs(c):
        if c == last:
            remote(*late_swap(1 - core)).wait_recv()
            packed, owning = rights_late[...].astype(jnp.float32), 1
        else:
            for k in range(1, devices):
                peer = (me + devices - k) % devices
                spot = rights.at[c, peer % 2 * chips + peer // 2]
                remote(spot, spot, right_send.at[c, k], right_recv.at[c, k], peer).wait_recv()
            packed, owning = rights[c].astype(jnp.float32), chips
        packed = packed.reshape(half, LANES)
        moved = pltpu.roll(packed, rank, 1)
        shape = (2 * owning, 1, fold // owning, LANES)
        both = jnp.concatenate([packed.reshape(shape), moved.reshape(shape)], axis=1)
        both = both.reshape(size, LANES)
        within = lax.broadcasted_iota(jnp.int32, (size, LANES), 1) < rank
        sides = jnp.concatenate(
            [jnp.where(within, both, 0.0), jnp.where(within, 0.0, pltpu.roll(both, rank, 1))],
            axis=0,
        ).astype(jnp.bfloat16)
        grads[...] += jnp.dot(spread[c], sides, preferred_element_type=jnp.float32)

    def query_rows(k):
        return qs.at[pl.ds(k * number, number), :]

    order = wavefront(chunks, steps)
    ahead = min(AHEAD, chunks)
    for c in range(ahead):
        begin(c)
    for c in range(chunks):
        start(*swap(c, core))
    pa_load.wait()
    pb_load.wait()
    for copy in mates:
        start(*copy)
    for k in range(1, groups):
        start(
            q_hbm, query_rows(groups - k), q_send.at[k], q_recv.at[k], None,
            (group + k) % groups,
        )
    for c in range(ahead):
        begin_mate(c)
    clear()
    tgt_load.wait()
    from_mate(0)
    from_mate(1)
    for c in range(chunks):
        prepare(c)

    def weights():
        w_load.wait()
        pin_load.wait()
        seg_load.wait()
        from_mate(2)

    tasks = [weights]
    ready = {c: own_loaders(c) for c in range(chunks)}

    def take(c, s):
        ready[c] += step_loaders(c, s)
        if s % 2 == 0 or s == steps - 1:
            tasks.append(functools.partial(consume, c, ready[c], s == 0))
            ready[c] = []
        if s == steps - 1:
            tasks.append(functools.partial(soften, c))
            if c == 0:
                tasks.append(push_hot)
            tasks.append(functools.partial(mark_docs, c))

    ends = []
    for n, (c, s) in enumerate(order[ahead:]):
        if s == 0:
            begin(c)
            begin_mate(c)
            continue
        arrive(c, s - 1)
        take(c, s - 1)
        if s == steps - 1:
            ends.append((n + 2, c))
        while ends and ends[0][0] <= n and len(ends) > 1:
            c = ends.pop(0)[1]
            arrive(c, steps - 1)
            take(c, steps - 1)
        for _ in range(3):
            if tasks and n >= HOLD:
                tasks.pop(0)()
    while len(ends) > 1:
        c = ends.pop(0)[1]
        arrive(c, steps - 1)
        take(c, steps - 1)
        while tasks:
            tasks.pop(0)()
    while tasks:
        tasks.pop(0)()
    for c in range(last - 1):
        reduce(c)
    sum_hot()
    arrive(last, steps - 1)
    consume(last, step_loaders(last, steps - 1))
    soften_late()
    mark_docs(last)
    if last > 0:
        reduce(last - 1)
    for c in range(last - 1):
        add_docs(c)
    settle_late()
    q_load.wait()
    for k in range(1, groups):
        remote(
            query_rows(k), query_rows(k), q_send.at[groups - k], q_recv.at[groups - k], None,
            (group + k) % groups,
        ).wait_recv()
    for c in range(max(last - 1, 0), chunks):
        add_docs(c)

    for p in range(rank // 2):
        flat[:, p * LANES : (p + 1) * LANES] = grads[p * docs : (p + 1) * docs, :].astype(
            jnp.bfloat16
        )
    mine = pl.ds(pl.multiple_of(group * docs, docs), docs)
    value = lax.dot_general(flat[...], qs[...], ACROSS, preferred_element_type=jnp.float32)
    for k in range(1, groups):
        scores[k] = value[:, k * number : (k + 1) * number]
        start(
            scores.at[k], out_ref.at[mine, :], group_send.at[k], group_recv.at[k], None,
            (group + k) % groups,
        )
    out_ref[mine, :] = value[:, 0:number]
    for k in range(1, groups):
        other = (group + groups - k) % groups
        theirs = out_ref.at[pl.ds(pl.multiple_of(other * docs, docs), docs), :]
        remote(
            theirs, theirs, group_send.at[k], group_recv.at[k], None, other
        ).wait_recv()
    for c in range(last):
        for k in range(1, chips):
            for copy in rs_copies(c, (chip + k) % chips):
                remote(*copy).wait_send()
    for copy in sent:
        copy.wait_send()


def attribution(devices, groups, hidden, weight, proj_in, proj_out, targets, segments, queries):
    tokens, depth = hidden.shape
    width, vocab = weight.shape
    rank = proj_in.shape[1]
    number = queries.shape[0]
    docs = DOC_V * devices
    chips, steps = devices // 2, devices // 4
    chunks = max(1, min(4, tokens // (2 * chips * BLOCK)))
    size = tokens // chunks
    half = size // 2
    block = half // chips
    hbm = pl.BlockSpec(memory_space=pl.ANY)
    dma = pltpu.SemaphoreType.DMA
    ring = dma((2, steps, chunks))
    once = dma((chunks,))
    sides = dma((2, chunks))
    peers = dma((chunks, chips))
    everyone = dma((chunks, devices))
    across = dma((groups,))
    f32, bf16 = jnp.float32, jnp.bfloat16
    return pl.pallas_call(
        functools.partial(kernel, devices, groups, chunks),
        out_shape=jax.ShapeDtypeStruct((groups * docs, number), f32),
        in_specs=[hbm] * 7,
        out_specs=pl.BlockSpec(memory_space=pltpu.VMEM),
        scratch_shapes=[
            pltpu.VMEM((tokens, depth), bf16),
            pltpu.VMEM((chips, tokens // 2, 2 * depth), bf16),
            pltpu.VMEM((2, width, vocab), bf16),
            pltpu.VMEM((rank, width), bf16),
            pltpu.VMEM((1, tokens), jnp.int32),
            pltpu.VMEM((1, tokens), jnp.int32),
            pltpu.VMEM((groups * number, rank * rank), bf16),
            pltpu.VMEM((tokens // 2, 2 * vocab), f32),
            pltpu.VMEM((chunks, 2, half, LANES), f32),
            pltpu.VMEM((tokens // 2, LANES), jnp.int32),
            pltpu.VMEM((LANES, 2 * vocab), bf16),
            pltpu.VMEM((LANES, 2 * vocab), bf16),
            pltpu.VMEM((tokens // 2, LANES), f32),
            pltpu.VMEM((LANES, size), f32),
            pltpu.VMEM((chunks, docs * rank // 2, 2 * size), bf16),
            pltpu.VMEM((chunks, half, LANES), bf16),
            pltpu.VMEM((chunks, chips, 1, LANES), f32),
            pltpu.VMEM((chunks, chips, block, LANES), bf16),
            pltpu.VMEM((chunks, chips, 1, LANES), f32),
            pltpu.VMEM((chunks, devices, block // 2, LANES), bf16),
            pltpu.VMEM((half // 2, LANES), bf16),
            pltpu.VMEM((chips, half // 2, LANES), bf16),
            pltpu.VMEM((half // 2, LANES), f32),
            pltpu.VMEM((half // 2, LANES), bf16),
            pltpu.VMEM((chips, half // 2, LANES), bf16),
            pltpu.VMEM((half // LANES, 8, LANES), f32),
            pltpu.VMEM((chips, half // LANES, 8, LANES), f32),
            pltpu.VMEM((2, half // 2, LANES), bf16),
            pltpu.VMEM((docs * rank // 2, LANES), f32),
            pltpu.VMEM((docs, rank * rank), bf16),
            pltpu.VMEM((groups, docs, number), f32),
            dma((8,)), ring, ring, sides, sides, once, once, dma((3,)), dma((3,)), once, once,
            peers, peers, peers, peers, everyone, everyone, dma((3, chips)), dma((3, chips)),
            dma(()), dma(()), across, across, across, across,
        ],
        compiler_params=pltpu.CompilerParams(
            collective_id=0, has_side_effects=True, vmem_limit_bytes=60 * 1024 * 1024
        ),
    )(
        hidden, weight, proj_in.T, proj_out.T, targets[None, :], segments, queries,
    )


def solution(mesh):
    devices, groups = mesh.shape["vocab"], mesh.shape["tok"]
    return jax.shard_map(
        functools.partial(attribution, devices, groups),
        mesh=mesh,
        in_specs=(
            P("tok", "vocab"),
            P(None, "vocab"),
            P(),
            P("vocab", None),
            P("tok"),
            P("tok", None),
            P(("vocab", "tok"), None),
        ),
        out_specs=P(None, ("vocab", "tok")),
        check_vma=False,
    )
```

time: 75 us -> 70.4 us (0.939)
  Pallas kernels: 73.4 us -> 68.9 us
    pallas_call x1, Pallas kernels: 73.4 us -> 68.9 us  [attribution(): pl.pallas_call(functools.partial(kernel, devices, groups, chunks), out_sh...]
where the time goes in v2:
time: 70.4 us; the launch traced here: 70.2 us
  Pallas kernels  68.9 us (98%)
  local copies, waits for them, and re-layouts  1.32 us (2%)
    pallas_call x1, Pallas kernels, attribution(): pl.pallas_call(functools.partial(kernel, devices, groups, chunks), out_sh...  68.9 us

profile of v2, /device:TPU:0, one launch (start us, length us, event | category | flops | bytes accessed | tf_op | source)
XLA Modules:
  0.0 70.2 jit_solution(6538040821293091870)
XLA Ops:
  0.0 68.9 %shard_map.73 = f32[32,64]{1,0:T(8,128)} custom-call(bf16[1024,256]{1,0:T(8,128)(2,1)} %h_hbm.1, bf16[4096,1024]{1,0:T(8,128)(2,1)} %w_hbm.1, bf16[64,4096]{1,0:T(8,128)(2,1)} %bitcast.3, bf16[64,1024]{1,0:T(8,128)(2,1)} %bitcast.4, s32[1,1024]{1,0:T(1,128)} %bitcast.5, s32[1,1024]{1,0:T(1,128)} %seg_hbm.1, bf16[64,4096]{1,0:T(8,128)(2,1)} %q_hbm.1), custom_call_target="tpu_custom_call" | custom-call | tf_op jit(solution)/shard_map/pallas_call | solution.py:628
  68.9 1.3 %copy.9 = f32[32,64]{1,0:T(8,128)} copy(f32[32,64]{1,0:T(8,128)} %shard_map.73) | data formatting | bytes 16384

commit v3 on v2

--- a/solution.py
+++ b/solution.py
@@ -530,7 +530,10 @@
             tasks.append(functools.partial(soften, c))
             if c == 0:
                 tasks.append(push_hot)
-            tasks.append(functools.partial(mark_docs, c))
+            if c < last - 1:
+                tasks.append(functools.partial(mark_docs, c))
+            if c == 1 and c < last:
+                tasks.append(sum_hot)
 
     ends = []
     for n, (c, s) in enumerate(order[ahead:]):
@@ -557,16 +560,18 @@
             tasks.pop(0)()
     while tasks:
         tasks.pop(0)()
-    for c in range(last - 1):
-        reduce(c)
-    sum_hot()
     arrive(last, steps - 1)
     consume(last, step_loaders(last, steps - 1))
     soften_late()
-    mark_docs(last)
+    if last == 1:
+        sum_hot()
+    for c in range(last - 1):
+        reduce(c)
+    for c in range(max(last - 1, 0), chunks):
+        mark_docs(c)
     if last > 0:
         reduce(last - 1)
-    for c in range(last - 1):
+    for c in range(last - 2):
         add_docs(c)
     settle_late()
     q_load.wait()
@@ -575,7 +580,7 @@
             query_rows(k), query_rows(k), q_send.at[groups - k], q_recv.at[groups - k], None,
             (group + k) % groups,
         ).wait_recv()
-    for c in range(max(last - 1, 0), chunks):
+    for c in range(max(last - 2, 0), chunks):
         add_docs(c)
 
     for p in range(rank // 2):

time: 70.4 us -> 70.1 us (level)
  no operation moved by 1% of the time
where the time goes in v3:
time: 70.1 us; the launch traced here: 69.8 us
  Pallas kernels  68.5 us (98%)
  local copies, waits for them, and re-layouts  1.32 us (2%)
    pallas_call x1, Pallas kernels, attribution(): pl.pallas_call(functools.partial(kernel, devices, groups, chunks), out_sh...  68.5 us

profile of v3, /device:TPU:0, one launch (start us, length us, event | category | flops | bytes accessed | tf_op | source)
XLA Modules:
  0.0 69.8 jit_solution(9753340153581576460)
XLA Ops:
  0.0 68.5 %shard_map.73 = f32[32,64]{1,0:T(8,128)} custom-call(bf16[1024,256]{1,0:T(8,128)(2,1)} %h_hbm.1, bf16[4096,1024]{1,0:T(8,128)(2,1)} %w_hbm.1, bf16[64,4096]{1,0:T(8,128)(2,1)} %bitcast.3, bf16[64,1024]{1,0:T(8,128)(2,1)} %bitcast.4, s32[1,1024]{1,0:T(1,128)} %bitcast.5, s32[1,1024]{1,0:T(1,128)} %seg_hbm.1, bf16[64,4096]{1,0:T(8,128)(2,1)} %q_hbm.1), custom_call_target="tpu_custom_call" | custom-call | tf_op jit(solution)/shard_map/pallas_call | solution.py:633
  68.5 1.3 %copy.9 = f32[32,64]{1,0:T(8,128)} copy(f32[32,64]{1,0:T(8,128)} %shard_map.73) | data formatting | bytes 16384
